TPU v7x, 256 devices: a whole 4x4x8 slice. The times are simulated.
256 devices in a mesh: ta: 16 (over x_lo, y, core), xyz: 16 (over x_hi, z).
Axes of the slice: x: 4 (x_hi: 2, x_lo: 2; x = x_hi * 2 + x_lo), y: 4, z: 8, core: 2. Of those that a mesh axis runs over, the one named last changes fastest.
Arguments:
- prop_one: bfloat16 [16, 2, 12, 12, 32768], P('ta', None, None, None, 'xyz'), may hold values from -1.796875 to 1.796875
- prop_two: bfloat16 [16, 2, 12, 12, 32768], P('ta', None, None, None, 'xyz'), may hold values from -1.796875 to 1.796875
Outputs:
- momentum_fields: float32 [16, 16, 2, 32768], P(None, 'ta', None, 'xyz')
All inputs are finite; a program needn't handle non-finite values.
Results may differ from a plain program's by a relative error of at most 0.0003.
Values sent between devices are 32-bit elements; how exact they have to be, the bound alone decides.
A program may use at most 128 MiB of HBM per device.

v0:
```python
import math

import jax
import jax.numpy as jnp
import numpy as np
from jax import lax
from jax.sharding import PartitionSpec as P

L = 32


spin_columns = [[3, 2, 1, 0], [3, 2, 1, 0], [2, 3, 0, 1], [2, 3, 0, 1]]
spin_phases = [[1j, 1j, -1j, -1j], [-1.0, 1.0, 1.0, -1.0], [1j, -1j, -1j, 1j], [1.0, 1.0, 1.0, 1.0]]
chiral_signs = [1.0, 1.0, -1.0, -1.0]


def cut_along(shard, dim, count):
    dims = shard.shape
    parts = shard.reshape(*dims[:dim], count, dims[dim] // count, *dims[dim + 1 :])
    return jnp.moveaxis(parts, dim, 0)


def joined_along(parts, dim):
    dims = list(parts.shape[1:])
    dims[dim] *= parts.shape[0]
    return jnp.moveaxis(parts, 0, dim).reshape(dims)


def exchange_both(shard, axis, axes, splits, concats):
    sizes = [lax.axis_size(a) for a in axes]
    parts = cut_along(shard, splits[0], sizes[0])
    parts = jnp.moveaxis(cut_along(parts, splits[1] + 1, sizes[1]), 0, 1)
    inside = parts.shape[2:]
    parts = parts.reshape(-1, *inside)
    parts = lax.all_to_all(parts, axis, split_axis=0, concat_axis=0, tiled=True)
    parts = joined_along(parts.reshape(*sizes, *inside), concats[0] + 1)
    return joined_along(parts, concats[1])


def vertex_parts():
    result = []
    for gamma_index in range(4):
        columns = spin_columns[gamma_index]
        phases = spin_phases[gamma_index]
        rows_list = [columns[a // 3] * 3 + a % 3 for a in range(12)]
        phase_list = [complex(phases[a // 3]) for a in range(12)]
        result.append((rows_list, phase_list))
    return (result, [chiral_signs[a // 3] for a in range(12)])


def contract(prop_a, prop_b):
    gammas, chirality = vertex_parts()
    left_real, left_imag, right_real, right_imag = ([], [], [], [])
    for rows_list, phase_list in gammas:
        pick_real = jnp.stack([prop_a[0, q] for q in rows_list])
        pick_imag = jnp.stack([prop_a[1, q] for q in rows_list])
        phase_real = jnp.asarray(np.array([p.real for p in phase_list]), jnp.bfloat16)[
            :, None, None
        ]
        phase_imag = jnp.asarray(np.array([p.imag for p in phase_list]), jnp.bfloat16)[
            :, None, None
        ]
        left_real.append(phase_real * pick_real - phase_imag * pick_imag)
        left_imag.append(phase_real * pick_imag + phase_imag * pick_real)
        col_real = jnp.stack([prop_b[0][:, q] for q in rows_list], axis=1)
        col_imag = jnp.stack([prop_b[1][:, q] for q in rows_list], axis=1)
        factor = np.array(
            [
                [phase_list[c] * chirality[rows_list[c]] * chirality[a] for c in range(12)]
                for a in range(12)
            ]
        )
        factor_real = jnp.asarray(factor.real, jnp.bfloat16)[:, :, None]
        factor_imag = jnp.asarray(factor.imag, jnp.bfloat16)[:, :, None]
        right_real.append(factor_real * col_real + factor_imag * col_imag)
        right_imag.append(factor_imag * col_real - factor_real * col_imag)
    left_rows = jnp.stack(left_real + left_imag).reshape(8, 144, -1)
    right_rows = jnp.stack(right_real + right_imag).reshape(8, 144, -1)
    products = jnp.einsum("mks,nks->mns", left_rows, right_rows, preferred_element_type=jnp.float32)
    real_sum = products[:4, :4] - products[4:, 4:]
    imag_sum = products[:4, 4:] + products[4:, :4]
    return jnp.stack([real_sum.reshape(16, -1), imag_sum.reshape(16, -1)], axis=1)


def dft_tables(length):
    positions = np.arange(length)
    turn_count = positions[:, None] * positions[None, :] % length
    angles = turn_count * (2.0 * math.pi / length)
    cosines = jnp.asarray(np.cos(angles) / math.sqrt(length), jnp.float32)
    sines = jnp.asarray(np.sin(angles) / math.sqrt(length), jnp.float32)
    return (cosines, sines)


def plane_dft(fields):
    cosines, sines = dft_tables(L)
    highest = lax.Precision.HIGHEST
    shape = fields.shape
    grid = fields.reshape(shape[:4] + (L, L))
    real_part = grid[:, :, 0]
    imag_part = grid[:, :, 1]

    def along_z(values, table):
        return jnp.einsum(
            "tfpyz,zk->tfpyk", values, table, precision=highest, preferred_element_type=jnp.float32
        )

    def along_y(values, table):
        return jnp.einsum(
            "tfpyz,yk->tfpkz", values, table, precision=highest, preferred_element_type=jnp.float32
        )

    mid_real = along_z(real_part, cosines) + along_z(imag_part, sines)
    mid_imag = along_z(imag_part, cosines) - along_z(real_part, sines)
    out_real = along_y(mid_real, cosines) + along_y(mid_imag, sines)
    out_imag = along_y(mid_imag, cosines) - along_y(mid_real, sines)
    return jnp.stack([out_real, out_imag], axis=2).reshape(shape)


def line_dft(data):
    length = data.shape[-2]
    cosines, sines = dft_tables(length)
    real_part = data[..., 0, :, :]
    imag_part = data[..., 1, :, :]

    def transform_rows(values, table):
        return jnp.einsum(
            "...xq,xk->...qk",
            values,
            table,
            precision=lax.Precision.HIGHEST,
            preferred_element_type=jnp.float32,
        )

    out_real = transform_rows(real_part, cosines) + transform_rows(imag_part, sines)
    out_imag = transform_rows(imag_part, cosines) - transform_rows(real_part, sines)
    stacked = jnp.stack([out_real, out_imag], axis=-3)
    return stacked.reshape(stacked.shape[:-2] + (stacked.shape[-2] * stacked.shape[-1],))


def on_device(prop_one, prop_two):
    fields = lax.map(
        lambda slice_pair: contract(slice_pair[0], slice_pair[1]), (prop_one, prop_two)
    )
    local_times, field_count, parts, slab = fields.shape
    planes = slab // (L * L)
    fields = plane_dft(fields.reshape(local_times, field_count, parts, planes, L * L))
    regrouped = exchange_both(fields, ("ta", "xyz"), ("ta", "xyz"), (1, 4), (0, 3))
    result = line_dft(regrouped)
    return result


def solution(mesh):
    placed = (P("ta", None, None, None, "xyz"), P("ta", None, None, None, "xyz"))
    return jax.shard_map(
        on_device, mesh=mesh, in_specs=placed, out_specs=P(None, "ta", None, "xyz"), check_vma=False
    )
```

profile of v0, /device:TPU:1, one launch (start us, length us, event | category | flops | bytes accessed | tf_op | source)
XLA Modules:
  0.0 146.7 jit_solution(13518687957666164569)
XLA Ops:
  0.0 4.4 %fusion.5 = (bf16[1,3,12,2048]{3,0,2,1:T(2,128)(2,1)S(1)}, bf16[1,3,12,2048]{3,0,2,1:T(2,128)(2,1)S(1)}, bf16[1,3,12,2048]{3,0,2,1:T(2,128)(2,1)S(1)}, bf16[1,3,...) fusion(bf16[2,12,12,2048]{3,0,2,1:T(2,128)(2,1)} %bitcast.98), kind=kLoop, calls=%fused_computation.56 | loop fusion | bytes 2359296 | tf_op jit(solution)/shard_map/while/body/eval_jaxpr/slice | solution.py:55
  4.4 3.0 %fusion.4 = (bf16[1,6,12,2048]{3,0,2,1:T(2,128)(2,1)}, bf16[1,6,12,2048]{3,0,2,1:T(2,128)(2,1)}, bf16[1,6,12,2048]{3,0,2,1:T(2,128)(2,1)}, bf16[1,6,12,2048]{3,0,2,1:T(2,128)(2,1)}) fusion(bf16[2,12,12,2048]{3,0,2,1:T(2,128)(2,1)S(1)} %bitcast.99), kind=kLoop, calls=%fused_computation.55 | loop fusion | bytes 2359296 | tf_op jit(solution)/shard_map/while/body/eval_jaxpr/slice | solution.py:55
  7.3 2.3 %fusion.6 = (bf16[1,1,12,12,2048]{4,1,3,2,0:T(2,128)(2,1)S(1)}, bf16[1,1,12,12,2048]{4,1,3,2,0:T(2,128)(2,1)S(1)}) fusion(bf16[1,2,12,12,2048]{4,1,3,2,0:T(2,128)(2,1)S(1)} %copy-done.1), kind=kLoop, calls=%fused_computation.57 | loop fusion | bytes 2359296 | tf_op jit(solution)/shard_map/while/body/eval_jaxpr/slice | solution.py:65
  9.7 0.8 copy_bitcast_fusion
  10.5 1.2 slice_bitcast_fusion.17
  11.7 0.9 slice_bitcast_fusion.3
  12.6 1.2 slice_bitcast_fusion.13
  13.8 1.0 slice_bitcast_fusion.1
  14.8 6.4 %maximum_reduce_fusion = (bf16[12,12,2048]{2,1,0:T(8,128)(2,1)S(1)}, bf16[12,12,2048]{2,1,0:T(8,128)(2,1)S(1)}) fusion(bf16[1,3,12,2048]{3,0,2,1:T(2,128)(2,1)S(1)} %get-tuple-element.54, bf16[1,3,12,2048]{3,0,2,1:T(2,128)(2,1)S(1)} %get-tuple-element.55, bf16[1,3,12,2048]{3,0,2,1:T(2,128)(2,1)S(1)} %get-tuple-element.56, ...), kind=kLoop, calls=%fused_computation.9 | loop fusion | flops 1769472 | bytes 2359296 | tf_op jit(solution)/shard_map/while/body/eval_jaxpr/stack | solution.py:55
  21.5 0.3 copy-done.26
  22.4 8.1 %maximum_reduce_fusion.2 = (bf16[12,12,2048]{2,1,0:T(8,128)(2,1)}, bf16[12,12,2048]{2,1,0:T(8,128)(2,1)S(1)}) fusion(bf16[1,6,12,2048]{3,0,2,1:T(2,128)(2,1)} %get-tuple-element.48, bf16[1,6,12,2048]{3,0,2,1:T(2,128)(2,1)} %get-tuple-element.45, bf16[1,6,12,2048]{3,0,2,1:T(2,128)(2,1)} %get-tuple-element.46, bf16[1,6,12,2048]{3,0,2,1:T(2,128)(2,1)} %get-tuple-element.47), kind=kLoop, calls=%fused_computation.11 | loop fusion | flops 589824 | bytes 2359296 | tf_op jit(solution)/shard_map/while/body/eval_jaxpr/stack | solution.py:55
  30.5 1.5 stack.170
  32.1 0.7 mul.656
  33.1 1.2 subtract_dynamic-update-slice_fusion.3
  34.3 1.1 subtract_dynamic-update-slice_fusion.2
  35.3 1.1 subtract_dynamic-update-slice_fusion.1
  36.4 1.0 subtract_dynamic-update-slice_fusion
  37.4 1.1 add_dynamic-update-slice_fusion.3
  38.5 1.1 add_dynamic-update-slice_fusion.2
  39.6 1.1 add_dynamic-update-slice_fusion.1
  40.7 1.1 add_dynamic-update-slice_fusion
  41.8 12.8 %copy.194 = bf16[8,144,2048]{1,0,2:T(8,128)(2,1)} copy(bf16[8,144,2048]{2,1,0:T(8,128)(2,1)} %add_dynamic-update-slice_fusion) | data formatting | bytes 9437184 | tf_op jit(solution)/shard_map/while/body/eval_jaxpr/stack | solution.py:77
  54.7 0.6 pad_maximum_fusion
  55.8 0.6 pad_maximum_fusion.1
  56.6 0.3 copy-done.2
  56.8 0.3 pad_maximum_fusion.2
  57.3 0.8 copy-done.3
  58.2 0.3 pad_maximum_fusion.3
  58.6 0.2 copy-done.22
  58.9 1.1 add_dynamic-update-slice_fusion.7
  60.0 1.1 add_dynamic-update-slice_fusion.6
  61.1 1.1 add_dynamic-update-slice_fusion.5
  62.2 1.1 add_dynamic-update-slice_fusion.4
  63.3 1.1 subtract_dynamic-update-slice_fusion.7
  64.4 1.1 subtract_dynamic-update-slice_fusion.6
  65.5 1.1 subtract_dynamic-update-slice_fusion.5
  66.6 1.1 subtract_dynamic-update-slice_fusion.4
  67.7 12.7 %copy.193 = bf16[8,144,2048]{1,0,2:T(8,128)(2,1)} copy(bf16[8,144,2048]{2,1,0:T(8,128)(2,1)} %subtract_dynamic-update-slice_fusion.4) | data formatting | bytes 9437184 | tf_op jit(solution)/shard_map/while/body/eval_jaxpr/stack | solution.py:78
  80.4 7.1 %convolution_bitcast_fusion = f32[8,8,2048]{0,1,2:T(8,128)S(1)} fusion(bf16[8,144,2048]{1,0,2:T(8,128)(2,1)} %copy.193, bf16[8,144,2048]{1,0,2:T(8,128)(2,1)} %copy.194), kind=kOutput, calls=%fused_computation.2 | convolution fusion | flops 37748736 | bytes 9961472 | tf_op jit(solution)/shard_map/while/body/eval_jaxpr/mks,nks->mns/dot_general | solution.py:79
  87.5 6.5 %slice_subtract_fusion = (f32[4,4,2048]{0,1,2:T(4,128)}, f32[4,4,2048]{0,1,2:T(4,128)}) fusion(f32[8,8,2048]{0,1,2:T(8,128)S(1)} %convolution_bitcast_fusion), kind=kLoop, calls=%fused_computation.1 | loop fusion | flops 65536 | bytes 786432 | tf_op jit(solution)/shard_map/while/body/eval_jaxpr/sub | solution.py:80
  93.9 3.5 %copy.195 = f32[4,4,2048]{2,1,0:T(4,128)S(1)} copy(f32[4,4,2048]{0,1,2:T(4,128)} %get-tuple-element.43) | data formatting | bytes 262144 | tf_op jit(solution)/shard_map/while/body/eval_jaxpr/sub | solution.py:80
  97.7 3.8 %copy.196 = f32[4,4,2048]{2,1,0:T(4,128)S(1)} copy(f32[4,4,2048]{0,1,2:T(4,128)} %get-tuple-element.44) | data formatting | bytes 262144 | tf_op jit(solution)/shard_map/while/body/eval_jaxpr/add | solution.py:81
  101.7 0.5 fusion.7
  102.2 0.6 fusion.9
  102.8 0.6 convolution_add_fusion.1
  103.4 1.0 fusion.8
  104.4 0.5 convolution_subtract_fusion.1
  104.9 1.0 fusion.10
  105.9 1.0 fusion.1
  107.3 1.0 fusion
  108.7 0.4 copy.204
  109.1 0.6 reshape.1654
  109.7 31.1 %all_to_all.5 = f32[256,1,256]{2,1,0:T(1,128)S(1)} all-to-all(f32[256,1,256]{2,1,0:T(1,128)S(1)} %reshape.1654), channel_id=1, replica_groups=mesh['ta'=16,'xyz'=16] {'ta','xyz'}, dimensions={0} | all-to-all | bytes 524288 | tf_op jit(solution)/shard_map/all_to_all | solution.py:35
  140.7 0.5 broadcast.488
  141.2 1.3 reduce.8
  142.5 0.3 reshape.1655
  142.9 0.3 copy.205
  143.2 0.4 fusion.2
  143.6 0.4 fusion.3
  144.0 0.4 convolution_add_fusion.2
  144.6 0.2 stack.177
  144.9 0.4 convolution_subtract_fusion.2
  145.5 0.2 stack.178
  145.8 0.9 copy.212
  (77 shorter events, 3.9 us)
Async XLA Ops:
  0.0 4.4 %copy-start = (bf16[1,2,12,12,2048]{4,1,3,2,0:T(2,128)(2,1)S(1)}, bf16[1,2,12,12,2048]{4,1,3,2,0:T(2,128)(2,1)}, u32[]{:S(2)}) copy-start(bf16[1,2,12,12,2048]{4,1,3,2,0:T(2,128)(2,1)} %param.22) | copy-start | bytes 3538948
  4.4 3.0 %copy-start.1 = (bf16[1,2,12,12,2048]{4,1,3,2,0:T(2,128)(2,1)S(1)}, bf16[1,2,12,12,2048]{4,1,3,2,0:T(2,128)(2,1)}, u32[]{:S(2)}) copy-start(bf16[1,2,12,12,2048]{4,1,3,2,0:T(2,128)(2,1)} %param.23) | copy-start | bytes 3538948
  21.2 0.7 copy-start.26
  21.2 0.8 copy-start.25
  21.3 1.0 copy-start.24
  30.5 2.4 %copy-start.23 = (bf16[12]{0:T(256)(128)(2,1)S(1)}, bf16[12]{0:T(256)(128)(2,1)}, u32[]{:S(2)}) copy-start(bf16[12]{0:T(256)(128)(2,1)} %constant.51.clone) | copy-start | bytes 76
  41.7 12.8 %copy-start.5 = (bf16[1,12,3,2048]{3,2,1,0:T(4,128)(2,1)S(1)}, bf16[1,12,3,2048]{3,2,1,0:T(4,128)(2,1)}, u32[]{:S(2)}) copy-start(bf16[1,12,3,2048]{3,2,1,0:T(4,128)(2,1)} %get-tuple-element.85) | copy-start | bytes 442372
  41.7 12.8 %copy-start.6 = (bf16[1,12,3,2048]{3,2,1,0:T(4,128)(2,1)S(1)}, bf16[1,12,3,2048]{3,2,1,0:T(4,128)(2,1)}, u32[]{:S(2)}) copy-start(bf16[1,12,3,2048]{3,2,1,0:T(4,128)(2,1)} %get-tuple-element.86) | copy-start | bytes 442372
  41.8 12.8 %copy-start.7 = (bf16[1,12,3,2048]{3,2,1,0:T(4,128)(2,1)S(1)}, bf16[1,12,3,2048]{3,2,1,0:T(4,128)(2,1)}, u32[]{:S(2)}) copy-start(bf16[1,12,3,2048]{3,2,1,0:T(4,128)(2,1)} %get-tuple-element.87) | copy-start | bytes 442372
  41.8 12.9 %copy-start.8 = (bf16[1,12,3,2048]{3,2,1,0:T(4,128)(2,1)S(1)}, bf16[1,12,3,2048]{3,2,1,0:T(4,128)(2,1)}, u32[]{:S(2)}) copy-start(bf16[1,12,3,2048]{3,2,1,0:T(4,128)(2,1)} %get-tuple-element.88) | copy-start | bytes 442372
  54.6 0.9 copy-start.9
  54.6 1.0 copy-start.10
  54.6 1.1 copy-start.11
  54.6 1.2 copy-start.12
  55.8 1.0 copy-start.2
  57.1 1.0 copy-start.3
  57.1 1.1 copy-start.4
  58.2 0.7 copy-start.22
  58.9 1.1 copy-start.17
  58.9 1.1 copy-start.21
  60.0 1.1 copy-start.20
  61.1 1.1 copy-start.18
  61.1 1.1 copy-start.19
  97.7 4.0 %copy-start.14 = (f32[32,32,1,1]{1,0,3,2:T(8,128)S(1)}, f32[32,32,1,1]{1,0,3,2:T(8,128)}, u32[]{:S(2)}) copy-start(f32[32,32,1,1]{1,0,3,2:T(8,128)} %constant.66) | copy-start | bytes 12292
  101.7 1.1 copy-start.13
  141.2 1.9 %copy-start.16 = (f32[32,32,1]{1,0,2:T(8,128)S(1)}, f32[32,32,1]{1,0,2:T(8,128)}, u32[]{:S(2)}) copy-start(f32[32,32,1]{1,0,2:T(8,128)} %constant.68) | copy-start | bytes 12292
  142.8 1.1 copy-start.15
where the time goes:
time: 148 us; the launch traced here: 147 us
  local copies, waits for them, and re-layouts  58.7 us (40%)
  other arithmetic  41.4 us (28%)
  blocking collectives  31.1 us (21%)
  matrix products  14.9 us (10%)
    all_to_all x1, blocking collectives, exchange_both(): parts = lax.all_to_all(parts, axis, split_axis=0, concat_axis=0, tiled=True)  31.1 us
    unnamed x14, other arithmetic  15.2 us
    another operation x2, other arithmetic, contract(): pick_real = jnp.stack([prop_a[0, q] for q in rows_list])  14.5 us
    another operation x1, local copies, waits for them, and re-layouts, contract(): left_rows = jnp.stack(left_real + left_imag).reshape(8, 144, -1)  12.8 us
    another operation x1, local copies, waits for them, and re-layouts, contract(): right_rows = jnp.stack(right_real + right_imag).reshape(8, 144, -1)  12.7 us
    slice x2, local copies, waits for them, and re-layouts, contract(): pick_real = jnp.stack([prop_a[0, q] for q in rows_list])  7.3 us
    dot_general x1, matrix products, contract(): jnp.einsum('mks,nks->mns', left_rows, right_rows, preferred_element_type=...  7.1 us
    sub x1, other arithmetic, contract(): real_sum = products[:4, :4] - products[4:, 4:]  6.49 us

commit v1 on v0

v1 whole, which is shorter than its diff:
```python
import functools

import jax
import jax.numpy as jnp
import numpy as np
from jax import lax
from jax.experimental import pallas as pl
from jax.experimental.pallas import tpu as pltpu
from jax.sharding import PartitionSpec as P

L = 32
MESH = pl.DeviceIdType.MESH
ENTRIES = 144
PITCH = 32

REVERSED = [3, 2, 1, 0]
SWAPPED = [2, 3, 0, 1]
LEFT_PHASE = [1j, -1.0, 1j, 1.0]
RIGHT_PHASE = [-1j, 1.0, -1j, -1.0]


def split_table(values):
    high = jnp.asarray(values, jnp.float32).astype(jnp.bfloat16)
    high_np = np.asarray(values, np.float32).astype(jnp.bfloat16).astype(np.float64)
    low = np.asarray(values - high_np, np.float32).astype(jnp.bfloat16)
    high = np.asarray(values, np.float32).astype(jnp.bfloat16)
    return high, low


def real_form(z):
    return np.stack([np.stack([z.real, -z.imag]), np.stack([z.imag, z.real])])


def fold_tables():
    result = []
    for chunk in range(2):
        table = np.zeros((2, 2, 4, 2, 8, 2, 8, 2, 8))
        for f8 in range(8):
            mu, nu = f8 // 2, 2 * chunk + f8 % 2
            phase = LEFT_PHASE[mu] * RIGHT_PHASE[nu]
            for parity in range(2):
                for m in range(4):
                    z = phase * np.exp(-2j * np.pi * np.arange(8) * (2 * m + parity) / 8)
                    form = real_form(z)
                    for x in range(2):
                        table[parity, :, m, x, f8, x, f8] = form
        result.append(np.concatenate(split_table(table.reshape(256, 256)), axis=0))
    return np.stack(result)


def twiddle_tables():
    kl = (2 * np.arange(4)[None, :] + np.arange(2)[:, None]).reshape(8)
    angle = 2 * np.pi * kl[:, None] * np.repeat(np.arange(4), 32)[None, :] / 32
    rows = np.stack([np.cos(angle), np.sin(angle)])
    return np.repeat(rows[:, :, None, :], 8, axis=2).reshape(2, 64, 128).astype(np.float32)


def plane_tables():
    yl, z = np.arange(4)[:, None], np.arange(32)[None, :]
    kz = np.array([4 * high + low for low in range(4) for high in range(8)])
    result = []
    for parity in range(2):
        table = np.zeros((2, 128, 2, 4, 32))
        for tile in range(2):
            for slot in range(4):
                part, kh = slot // 2, 2 * tile + (slot % 2 if parity == 0 else 1 - slot % 2)
                w = np.exp(-2j * np.pi * ((yl * kh / 4)[:, :, None] + z[:, :, None] * kz[None, None, :] / 32)) / 32
                form = real_form(w.reshape(128, 32))
                table[:, :, tile, slot] = form[part]
        result.append(np.stack(split_table(table.reshape(256, 256))))
    return np.stack(result)


def line_tables():
    w = np.exp(-2j * np.pi * np.arange(32)[:, None] * np.arange(32)[None, :] / 32) / np.sqrt(32)
    form = real_form(w)
    table = np.zeros((2, 4, 32, 2, 4, 32))
    for f4 in range(4):
        table[:, f4, :, :, f4] = form.transpose(1, 2, 0, 3)
    return np.stack(split_table(table.reshape(256, 256)))


def split_values(values):
    high = values.astype(jnp.bfloat16)
    low = (values - high.astype(jnp.float32)).astype(jnp.bfloat16)
    return high, low


def dot(a, b):
    return jnp.dot(a, b, preferred_element_type=jnp.float32)


def wide_dot(values, high_table, low_table):
    rows = values.shape[0]
    high, low = split_values(values)
    both = dot(jnp.concatenate([high, low], axis=0), high_table)
    return both[:rows] + both[rows:] + dot(high, low_table)


def widen(chunk, staged, sites):
    rows = 36 * PITCH
    base = chunk * rows

    def one(index, carry):
        start = pl.multiple_of(base + index * 128, 128)
        sites[pl.ds(start, 128), :] = staged[pl.ds(start, 128), :].astype(jnp.float32)
        return carry

    lax.fori_loop(0, rows // 128, one, 0)


def contract_half(chunk, sites, fields):
    right_pair = [REVERSED, SWAPPED][chunk]

    def one_plane(h, carry):
        def entry(prop, part, row, column):
            start = (prop * ENTRIES + row * 12 + column) * PITCH + part
            return sites[pl.ds(start + 16 * h, 8, stride=2), :]

        by_spin = []
        for t in range(4):
            sums = [[None] * 4 for _ in range(2)]
            for i in range(3):
                for k in range(3):
                    first = [[entry(0, part, 3 * s + i, 3 * t + k) for part in range(2)] for s in range(4)]
                    second = [[entry(1, part, 3 * s + i, 3 * right_pair[t] + k) for part in range(2)] for s in range(4)]
                    for side, pair in enumerate((REVERSED, SWAPPED)):
                        for s in range(4):
                            ar, ai = first[pair[s]]
                            br, bi = second[s]
                            re = ar * br + ai * bi
                            im = ai * br - ar * bi
                            if sums[side][s] is None:
                                sums[side][s] = [re, im]
                            else:
                                sums[side][s] = [sums[side][s][0] + re, sums[side][s][1] + im]
            left = []
            for part in range(2):
                p0, p1, p2, p3 = [sums[0][s][part] for s in range(4)]
                even, odd = p0 + p2, p1 + p3
                q0, q1, q2, q3 = [sums[1][s][part] for s in range(4)]
                outer, inner = q0 - q3, q1 - q2
                left.append([even + odd, even - odd, outer - inner, outer + inner])
            by_spin.append(left)
        for mu in range(4):
            for part in range(2):
                p0, p1, p2, p3 = [by_spin[t][part][mu] for t in range(4)]
                if chunk == 0:
                    even, odd = p0 + p2, p1 + p3
                    pair = (even + odd, even - odd)
                else:
                    outer, inner = p0 - p3, p1 - p2
                    pair = (outer - inner, outer + inner)
                for side in range(2):
                    row = ((2 * mu + side) * 2 + part) * 8
                    fields[pl.ds(pl.multiple_of(h * 128, 128) + row, 8), :] = pair[side]
        return carry

    lax.fori_loop(0, 2, one_plane, 0)


def plane_transform(chunk, fields, fold_ref, twiddle_ref, plane_ref, put):
    high, low = split_values(fields[...])
    folded = dot(fold_ref[chunk], jnp.concatenate([high, low], axis=1))
    folded = folded[:256, :128] + folded[:256, 128:] + folded[256:, :128]
    halves = []
    for parity in range(2):
        re = folded[parity * 128 : parity * 128 + 64].reshape(4, 2, 8, 128)
        im = folded[parity * 128 + 64 : parity * 128 + 128].reshape(4, 2, 8, 128)
        cosines = twiddle_ref[0, parity * 32 : parity * 32 + 32, :].reshape(4, 1, 8, 128)
        sines = twiddle_ref[1, parity * 32 : parity * 32 + 32, :].reshape(4, 1, 8, 128)
        turned = jnp.concatenate(
            [(re * cosines + im * sines).reshape(64, 128), (im * cosines - re * sines).reshape(64, 128)], axis=1
        )
        halves.append(wide_dot(turned, plane_ref[parity, 0], plane_ref[parity, 1]))
    even_slot = (lax.broadcasted_iota(jnp.int32, (64, 128), 1) // 32) % 2 == 0
    for tile in range(2):
        a = halves[0][:, tile * 128 : (tile + 1) * 128]
        b = halves[1][:, tile * 128 : (tile + 1) * 128]
        put(2 * tile, jnp.where(even_slot, a, b))
        put(2 * tile + 1, jnp.where(even_slot, b, a))


def field_kernel(
    one_ref, two_ref, fold_hbm, twiddle_hbm, plane_hbm, out_ref, staged, sites, fields, fold_ref, twiddle_ref, plane_ref, sems
):
    copies = []
    for chunk in range(8):
        rows = 36 * PITCH
        source = (one_ref, two_ref)[chunk // 4]
        copies.append(
            pltpu.make_async_copy(
                source.at[pl.ds((chunk % 4) * rows, rows)], staged.at[pl.ds(chunk * rows, rows)], sems.at[chunk]
            )
        )
        copies[-1].start()
    tables = [
        pltpu.make_async_copy(source, target, sems.at[8 + index])
        for index, (source, target) in enumerate(
            ((fold_hbm, fold_ref), (twiddle_hbm, twiddle_ref), (plane_hbm, plane_ref))
        )
    ]
    for table in tables:
        table.start()
    for chunk in range(8):
        copies[chunk].wait()
        widen(chunk, staged, sites)
    for chunk in range(2):
        contract_half(chunk, sites, fields)
        if chunk == 0:
            for table in tables:
                table.wait()

        def put(kh, rows):
            out_ref[chunk, 4 * kh : 4 * kh + 4] = rows.reshape(4, 16, 128)

        plane_transform(chunk, fields, fold_ref, twiddle_ref, plane_ref, put)


def line_transform(held, flip, line_ref, staging, chunk):
    turned = []
    for g in range(2):
        block = jnp.concatenate([held[chunk, pl.ds(4 * g + f4, 32, stride=8), :] for f4 in range(4)], axis=0)
        across = block.T
        turned.append(jnp.concatenate([across[:64], across[64:]], axis=1))
    result = wide_dot(jnp.concatenate(turned, axis=0), line_ref[0], line_ref[1])
    lane = lax.broadcasted_iota(jnp.int32, (8, 128), 1)
    low_half, even_slot = lane < 64, (lane // 32) % 2 == 0
    for g in range(2):
        for k in range(2):
            for part in range(2):
                v = [
                    result[((g * 2 + k) * 4 + j) * 8 : ((g * 2 + k) * 4 + j + 1) * 8, part * 128 : (part + 1) * 128]
                    for j in range(4)
                ]
                w = [None] * 4
                for j in range(2):
                    w[j] = jnp.where(low_half, v[j], pltpu.roll(v[j + 2], 64, 1))
                    w[j + 2] = jnp.where(low_half, pltpu.roll(v[j], 64, 1), v[j + 2])
                for j in (0, 2):
                    first = jnp.where(even_slot, w[j], pltpu.roll(w[j + 1], 32, 1))
                    second = jnp.where(even_slot, pltpu.roll(w[j], 96, 1), w[j + 1])
                    start = pl.multiple_of(16 * lax.rem(k + flip, 2), 16) + part
                    staging[8 * chunk + 4 * g + j, pl.ds(start, 8, stride=2), :] = first
                    staging[8 * chunk + 4 * g + j + 1, pl.ds(start, 8, stride=2), :] = second


def exchange_kernel(fields_ref, line_ref, out_ref, held, staging, send_sems, recv_sems, last_send, last_recv, own_sems):
    ta, me = lax.axis_index("ta"), lax.axis_index("xyz")
    barrier = pltpu.get_barrier_semaphore()

    def greet(offset, carry):
        pl.semaphore_signal(
            barrier, inc=1, device_id={"xyz": lax.rem(me + offset, 16)}, device_id_type=MESH
        )
        pl.semaphore_signal(
            barrier, inc=1, device_id={"ta": lax.rem(ta + offset, 16)}, device_id_type=MESH
        )
        return carry

    lax.fori_loop(1, 16, greet, 0)
    pl.semaphore_wait(barrier, 30)

    def crossing(chunk, source, target, peer):
        return pltpu.make_async_remote_copy(
            src_ref=fields_ref.at[chunk, target],
            dst_ref=held.at[chunk, pl.ds(pl.multiple_of(source * 16, 16), 16)],
            send_sem=send_sems.at[chunk, target],
            recv_sem=recv_sems.at[chunk, source],
            device_id={"xyz": peer},
            device_id_type=MESH,
        )

    for chunk in range(2):

        def send(offset, carry, chunk=chunk):
            q = lax.rem(me + offset, 16)
            crossing(chunk, me, q, q).start()
            return carry

        lax.fori_loop(1, 16, send, 0)
        held[chunk, pl.ds(pl.multiple_of(me * 16, 16), 16), :] = fields_ref[chunk, me]

    flip = lax.rem(me // 4, 2)

    def leaving(f, f16, source):
        return pltpu.make_async_remote_copy(
            src_ref=staging.at[f16],
            dst_ref=out_ref.at[source],
            send_sem=last_send.at[f16],
            recv_sem=last_recv.at[source],
            device_id={"ta": f},
            device_id_type=MESH,
        )

    for chunk in range(2):

        def arrive(offset, carry, chunk=chunk):
            q = lax.rem(me + offset, 16)
            crossing(chunk, q, me, q).wait_recv()
            return carry

        lax.fori_loop(1, 16, arrive, 0)
        line_transform(held, flip, line_ref, staging, chunk)
        for f8 in range(8):
            f = 4 * (f8 // 2) + 2 * chunk + f8 % 2

            @pl.when(f != ta)
            def _(f=f, f16=8 * chunk + f8):
                leaving(f, f16, ta).start()

            @pl.when(f == ta)
            def _(f16=8 * chunk + f8):
                pltpu.make_async_copy(staging.at[f16], out_ref.at[ta], own_sems.at[0]).start()

    for chunk in range(2):

        def sent(offset, carry, chunk=chunk):
            q = lax.rem(me + offset, 16)
            crossing(chunk, me, q, q).wait_send()
            return carry

        lax.fori_loop(1, 16, sent, 0)
        for f8 in range(8):
            f = 4 * (f8 // 2) + 2 * chunk + f8 % 2

            @pl.when(f != ta)
            def _(f=f, f16=8 * chunk + f8):
                leaving(f, f16, ta).wait_send()

    pltpu.make_async_copy(staging.at[0], out_ref.at[ta], own_sems.at[0]).wait()

    def final(offset, carry):
        t = lax.rem(ta + offset, 16)
        leaving(t, 0, t).wait_recv()
        return carry

    lax.fori_loop(1, 16, final, 0)


def site_rows(prop):
    entries = prop.transpose(0, 2, 3, 1, 4).reshape(ENTRIES, 2, 16, 128)
    return entries.transpose(0, 2, 1, 3).reshape(ENTRIES * PITCH, 128)


def on_device(prop_one, prop_two):
    vmem, anywhere = pl.BlockSpec(memory_space=pltpu.VMEM), pl.BlockSpec(memory_space=pl.ANY)
    fields = pl.pallas_call(
        field_kernel,
        name="fields",
        out_shape=jax.ShapeDtypeStruct((2, 16, 16, 128), jnp.float32),
        in_specs=[anywhere] * 5,
        out_specs=vmem,
        scratch_shapes=[
            pltpu.VMEM((2 * ENTRIES * PITCH, 128), jnp.bfloat16),
            pltpu.VMEM((2 * ENTRIES * PITCH, 128), jnp.float32),
            pltpu.VMEM((256, 128), jnp.float32),
            pltpu.VMEM((2, 512, 256), jnp.bfloat16),
            pltpu.VMEM((2, 64, 128), jnp.float32),
            pltpu.VMEM((2, 2, 256, 256), jnp.bfloat16),
            pltpu.SemaphoreType.DMA((11,)),
        ],
        compiler_params=pltpu.CompilerParams(vmem_limit_bytes=67_043_328),
        cost_estimate=pl.CostEstimate(flops=20_000_000, bytes_accessed=4_000_000, transcendentals=0),
    )(site_rows(prop_one), site_rows(prop_two), jnp.asarray(fold_tables()), jnp.asarray(twiddle_tables()), jnp.asarray(plane_tables()))
    rows = pl.pallas_call(
        exchange_kernel,
        name="exchange",
        out_shape=jax.ShapeDtypeStruct((16, 32, 128), jnp.float32),
        in_specs=[vmem, vmem],
        out_specs=anywhere,
        scratch_shapes=[
            pltpu.VMEM((2, 256, 128), jnp.float32),
            pltpu.VMEM((16, 32, 128), jnp.float32),
            pltpu.SemaphoreType.DMA((2, 16)),
            pltpu.SemaphoreType.DMA((2, 16)),
            pltpu.SemaphoreType.DMA((16,)),
            pltpu.SemaphoreType.DMA((16,)),
            pltpu.SemaphoreType.DMA((1,)),
        ],
        compiler_params=pltpu.CompilerParams(collective_id=0, has_side_effects=True, vmem_limit_bytes=16 << 20),
    )(fields, jnp.asarray(line_tables()))
    return rows.reshape(16, 16, 2, 128).transpose(0, 2, 1, 3).reshape(16, 1, 2, 2048)


def solution(mesh):
    placed = (P("ta", None, None, None, "xyz"), P("ta", None, None, None, "xyz"))
    return jax.shard_map(
        on_device, mesh=mesh, in_specs=placed, out_specs=P(None, "ta", None, "xyz"), check_vma=False
    )
```

time: 148 us -> 32 us (0.22)
  the two profiles are of different devices: /device:TPU:1 before, /device:TPU:9 now
where the time goes in v1:
time: 32 us; the launch traced here: 31.6 us
  Pallas kernels  29 us (91%)
  local copies, waits for them, and re-layouts  2.6 us (8%)
    pallas_call x1, Pallas kernels, on_device(): pl.pallas_call(exchange_kernel, name='exchange', out_shape=jax.ShapeDtype...  23.2 us
    pallas_call x1, Pallas kernels, on_device(): pl.pallas_call(field_kernel, name='fields', out_shape=jax.ShapeDtypeStruc...  5.83 us
    unnamed x5, local copies, waits for them, and re-layouts  2.6 us

profile of v1, /device:TPU:9, one launch (start us, length us, event | category | flops | bytes accessed | tf_op | source)
XLA Modules:
  0.0 31.6 jit_solution(3943252238109316879)
XLA Ops:
  0.0 5.8 %fields.1.fields_ref = f32[2,16,16,128]{3,2,1,0:T(8,128)} custom-call(bf16[4608,128]{1,0:T(8,128)(2,1)} %bitcast.20, bf16[4608,128]{1,0:T(8,128)(2,1)} %bitcast.21, bf16[2,512,256]{2,1,0:T(8,128)(2,1)} %constant.8.clone.fold_hbm, f32[2,64,128]{2,1,0:T(8,128)} %constant.9.clone.twiddle_hbm, bf16[2,2,256,256]{3,2,1,0:T(8,128)(2,1)} %constant.10.clone.plane_hbm), custom_call_target="tpu_custom_call" | custom-call | flops 20000000 | bytes 4000000 | tf_op jit(solution)/shard_map/fields/pallas_call | solution.py:348
  5.8 0.0 copy-start
  5.8 0.9 %copy-done = f32[2,16,16,128]{3,2,1,0:T(8,128)S(1)} copy-done((f32[2,16,16,128]{3,2,1,0:T(8,128)S(1)}, f32[2,16,16,128]{3,2,1,0:T(8,128)}, u32[]{:S(2)}) %copy-start) | copy-done | bytes 262168
  6.8 0.0 copy-start.1
  6.8 0.9 %copy-done.1 = bf16[2,256,256]{2,1,0:T(8,128)(2,1)S(1)} copy-done((bf16[2,256,256]{2,1,0:T(8,128)(2,1)S(1)}, bf16[2,256,256]{2,1,0:T(8,128)(2,1)}, u32[]{:S(2)}) %copy-start.1) | copy-done | bytes 262168
  7.7 23.2 %exchange.1 = f32[16,32,128]{2,1,0:T(8,128)S(1)} custom-call(f32[2,16,16,128]{3,2,1,0:T(8,128)S(1)} %copy-done, bf16[2,256,256]{2,1,0:T(8,128)(2,1)S(1)} %copy-done.1), custom_call_target="tpu_custom_call" | custom-call | tf_op jit(solution)/shard_map/exchange/pallas_call | solution.py:366
  30.9 0.7 %copy.11 = f32[16,1,2,2048]{3,2,1,0:T(2,128)} copy(f32[16,1,2,2048]{3,2,1,0:T(2,128)S(1)} %bitcast.19) | data formatting | bytes 524288
Async XLA Ops:
  5.8 1.0 %copy-start = (f32[2,16,16,128]{3,2,1,0:T(8,128)S(1)}, f32[2,16,16,128]{3,2,1,0:T(8,128)}, u32[]{:S(2)}) copy-start(f32[2,16,16,128]{3,2,1,0:T(8,128)} %fields.1.fields_ref) | copy-start | bytes 786436
  6.8 0.9 %copy-start.1 = (bf16[2,256,256]{2,1,0:T(8,128)(2,1)S(1)}, bf16[2,256,256]{2,1,0:T(8,128)(2,1)}, u32[]{:S(2)}) copy-start(bf16[2,256,256]{2,1,0:T(8,128)(2,1)} %constant.11.clone.line_ref) | copy-start | bytes 786436
